TPU v7x, 32 devices: a whole 2x2x4 slice. The times are simulated.
32 devices in a mesh: expert: 4 (over x, core), shard: 8 (over z, y).
Axes of the slice: x: 2, y: 2, z: 4, core: 2. Of those that a mesh axis runs over, the one named last changes fastest.
Arguments:
- train_down: float32 [16, 6400, 4096], P('expert', None, 'shard'), may hold values from -0.109375 to 0.109375
- other_down: bfloat16 [16, 6400, 4096], P('expert', None, 'shard'), may hold values from -0.0390625 to 0.0390625
- router_weight: float32 [4096, 16], P('shard', 'expert'), may hold values from -0.09375 to 0.09375
- router_gain: float32 [4096], P('shard'), may hold values from 0.25 to 1.75
Outputs:
- ready_down: bfloat16 [16, 6400, 4096], P('expert', 'shard')
- scale_down: float32 [16, 6400], P('expert', 'shard')
- serve_router: bfloat16 [4096, 16], replicated
All inputs are finite; a program needn't handle non-finite values. Where the computation divides by a largest or mean magnitude, that divisor is 1e-20 or more.
Results may differ from a plain program's by a relative error of at most 0.001.
Values may be sent and summed in bfloat16 or wider, within the bound.
A program may use at most 256 MiB of HBM per device.

v0:
```python
import functools

import jax
import jax.numpy as jnp
from jax import lax
from jax.experimental import pallas as pl
from jax.experimental.pallas import tpu as pltpu
from jax.sharding import PartitionSpec as P

MESH = pl.DeviceIdType.MESH
AHEAD = 2
LANES = 128


def kernel(
    groups, shards, parts,
    train, other, router, gain,
    ready, scale_out, serve,
    tbuf, obuf, stage, lmax, rmax, gown, gmax, rparts, rflip,
    tsem, osem, own_sem, data_send, data_recv, rs_send, rs_recv, ag_send, ag_recv,
    r1_send, r1_recv, r2_send, r2_recv,
):
    me = lax.axis_index("shard")
    group = lax.axis_index("expert")
    experts = train.shape[0]
    slots, _, rows, cols = tbuf.shape
    chunks = experts * parts
    block = rows * parts

    def shard_id(k):
        return lax.rem(me + k, shards)

    def group_id(k):
        return lax.rem(group + k, groups)

    barrier = pltpu.get_barrier_semaphore()
    for k in range(1, shards):
        pl.semaphore_signal(barrier, inc=1, device_id=(group, shard_id(k)), device_id_type=MESH)
    for k in range(1, groups):
        pl.semaphore_signal(barrier, inc=1, device_id=(group_id(k), me), device_id_type=MESH)

    def place(c, d):
        return c // parts, pl.ds(pl.multiple_of(d * block + lax.rem(c, parts) * rows, 8), rows)

    def load(c, d):
        e, span = place(c, d)
        slot = lax.rem(c, slots)
        return (
            pltpu.make_async_copy(train.at[e, span], tbuf.at[slot, d], tsem.at[slot, d]),
            pltpu.make_async_copy(other.at[e, span], obuf.at[slot, d], osem.at[slot, d]),
        )

    def start_load(c):
        def one(d, _):
            for copy in load(c, d):
                copy.start()
            return 0
        lax.fori_loop(0, shards, one, 0)

    def columns_of(d):
        return pl.ds(pl.multiple_of(d * cols, LANES), cols)

    def send(src, dst, send_sem, recv_sem, peer):
        return pltpu.make_async_remote_copy(
            src_ref=src, dst_ref=dst, send_sem=send_sem, recv_sem=recv_sem,
            device_id=(group, peer), device_id_type=MESH,
        )

    def data_copy(c, d):
        e = c // parts
        span = pl.ds(pl.multiple_of(lax.rem(c, parts) * rows, 8), rows)
        return stage.at[c, d], ready.at[e, span, columns_of(me)]

    start_load(0)
    start_load(1)
    pl.semaphore_wait(barrier, shards - 1 + groups - 1)

    rparts[group, me] = router[...] * gain[...]
    for k in range(1, shards):
        send(rparts.at[group, me], rparts.at[group, me], r1_send, r1_recv, shard_id(k)).start()

    def find_max(c):
        slot = lax.rem(c, slots)

        def one(d, _):
            for copy in load(c, d):
                copy.wait()
            best = None
            for j in range(0, cols, LANES):
                at = pl.ds(j, LANES)
                now = jnp.abs(tbuf[slot, d, :, at] + obuf[slot, d, :, at].astype(jnp.float32))
                best = now if best is None else jnp.maximum(best, now)
            lmax[c, d] = jnp.max(best.T, axis=0, keepdims=True)
            return 0
        lax.fori_loop(0, shards, one, 0)

        def tell(k, _):
            peer = shard_id(k)
            send(lmax.at[c, peer], rmax.at[c, me], rs_send.at[c], rs_recv.at[c], peer).start()
            return 0
        lax.fori_loop(1, shards, tell, 0)
        rmax[c, me] = lmax[c, me]

    def merge(c):
        some = rmax.at[c, pl.ds(0, shards - 1)]
        pltpu.make_async_copy(some, some, rs_recv.at[c]).wait()
        best = rmax[c, 0]
        for d in range(1, shards):
            best = jnp.maximum(best, rmax[c, d])
        gown[c] = best
        scale_out[c] = best

        def tell(k, _):
            send(gown.at[c], gmax.at[c, me], ag_send.at[c], ag_recv.at[c], shard_id(k)).start()
            return 0
        lax.fori_loop(1, shards, tell, 0)
        gmax[c, me] = best

    def narrow(c):
        slot = lax.rem(c, slots)
        some = gmax.at[c, pl.ds(0, shards - 1)]
        pltpu.make_async_copy(some, some, ag_recv.at[c]).wait()

        def one(k, _):
            d = lax.rem(me + shards // 2 + k, shards)
            tall = jnp.broadcast_to(gmax[c, d], (LANES, rows)).T
            for j in range(0, cols, LANES):
                at = pl.ds(j, LANES)
                now = tbuf[slot, d, :, at] + obuf[slot, d, :, at].astype(jnp.float32)
                stage[c, d, :, at] = (now / tall).astype(jnp.bfloat16)
            src, dst = data_copy(c, d)

            @pl.when(d != me)
            def _():
                send(src, dst, data_send.at[d], data_recv.at[me], d).start()

            @pl.when(d == me)
            def _():
                pltpu.make_async_copy(src, dst, own_sem).start()
            return 0
        lax.fori_loop(0, shards, one, 0)

    def step(c, _):
        @pl.when(c < chunks)
        def _():
            find_max(c)

        @pl.when((c >= 1) & (c <= chunks))
        def _():
            merge(c - 1)

        @pl.when(c >= AHEAD)
        def _():
            narrow(c - AHEAD)

        @pl.when(c + 2 < chunks)
        def _():
            start_load(c + 2)
        return 0

    lax.fori_loop(0, chunks + AHEAD, step, 0)

    some = rparts.at[0, pl.ds(0, shards - 1)]
    pltpu.make_async_copy(some, some, r1_recv).wait()
    for k in range(1, groups):
        pltpu.make_async_remote_copy(
            src_ref=rparts.at[group], dst_ref=rparts.at[group], send_sem=r2_send, recv_sem=r2_recv,
            device_id=(group_id(k), me), device_id_type=MESH,
        ).start()
    some = rparts.at[pl.ds(0, groups - 1)]
    pltpu.make_async_copy(some, some, r2_recv).wait()
    wide = router.shape[1]
    for d in range(shards):
        for g in range(groups):
            rflip[g * experts:(g + 1) * experts, :] = rparts[g, d]
        serve[d * wide:(d + 1) * wide, :] = rflip[...].T.astype(jnp.bfloat16)

    some = rparts.at[0, pl.ds(0, shards - 1)]
    pltpu.make_async_copy(some, some, r1_send).wait()
    some = rparts.at[pl.ds(0, groups - 1)]
    pltpu.make_async_copy(some, some, r2_send).wait()

    def drain(c, _):
        some = rmax.at[c, pl.ds(0, shards - 1)]
        pltpu.make_async_copy(some, some, rs_send.at[c]).wait()
        pltpu.make_async_copy(some, some, ag_send.at[c]).wait()
        return 0
    lax.fori_loop(0, chunks, drain, 0)

    mine = ready.at[:, :, columns_of(me)]
    pltpu.make_async_copy(mine, mine, own_sem).wait()

    def finish(k, _):
        d = shard_id(k)
        there = ready.at[:, :, columns_of(d)]
        pltpu.make_async_copy(there, there, data_send.at[d]).wait()
        pltpu.make_async_copy(there, there, data_recv.at[d]).wait()
        return 0
    lax.fori_loop(1, shards, finish, 0)


def pieces(block):
    for count in (5, 4, 3, 2):
        if block % (16 * count) == 0:
            return count
    return 1


def per_device(groups, shards, train_down, other_down, router_weight, router_gain):
    experts, height, cols = train_down.shape
    block = height // shards
    parts = pieces(block)
    rows = block // parts
    chunks = experts * parts
    slots = AHEAD + 2
    wide = router_weight.shape[0]
    f32, bf16 = jnp.float32, jnp.bfloat16
    dma = pltpu.SemaphoreType.DMA
    hbm = pl.BlockSpec(memory_space=pl.ANY)
    vmem = pl.BlockSpec(memory_space=pltpu.VMEM)
    ready, scale, serve = pl.pallas_call(
        functools.partial(kernel, groups, shards, parts),
        out_shape=(
            jax.ShapeDtypeStruct((experts, block, cols * shards), bf16),
            jax.ShapeDtypeStruct((chunks, 1, rows), f32),
            jax.ShapeDtypeStruct((wide * shards, experts * groups), bf16),
        ),
        in_specs=[hbm, hbm, vmem, vmem],
        out_specs=(hbm, vmem, vmem),
        scratch_shapes=[
            pltpu.VMEM((slots, shards, rows, cols), f32),
            pltpu.VMEM((slots, shards, rows, cols), bf16),
            pltpu.VMEM((chunks, shards, rows, cols), bf16),
            pltpu.VMEM((chunks, shards, 1, rows), f32),
            pltpu.VMEM((chunks, shards, 1, rows), f32),
            pltpu.VMEM((chunks, 1, rows), f32),
            pltpu.VMEM((chunks, shards, 1, rows), f32),
            pltpu.VMEM((groups, shards, experts, wide), f32),
            pltpu.VMEM((groups * experts, wide), f32),
            dma((slots, shards)), dma((slots, shards)), dma(()),
            dma((shards,)), dma((shards,)),
            dma((chunks,)), dma((chunks,)), dma((chunks,)), dma((chunks,)),
            dma(()), dma(()), dma(()), dma(()),
        ],
        compiler_params=pltpu.CompilerParams(
            collective_id=0, has_side_effects=True, vmem_limit_bytes=62 * 2**20
        ),
    )(train_down, other_down, router_weight.T, router_gain[None, :])
    return ready, scale.reshape(experts, block), serve


def solution(mesh):
    in_specs = (
        P("expert", None, "shard"),
        P("expert", None, "shard"),
        P("shard", "expert"),
        P("shard"),
    )
    out_specs = (P("expert", "shard", None), P("expert", "shard"), P())
    body = functools.partial(per_device, mesh.shape["expert"], mesh.shape["shard"])
    return jax.shard_map(
        body, mesh=mesh, in_specs=in_specs, out_specs=out_specs, check_vma=False
    )
```

profile of v0, /device:TPU:0, one launch (start us, length us, event | category | flops | bytes accessed | tf_op | source)
XLA Modules:
  0.0 608.7 jit_solution(12104473608895775337)
XLA Ops:
  0.6 586.4 %shard_map.67 = (bf16[4,800,4096]{2,1,0:T(8,128)(2,1)}, f32[20,1,160]{2,1,0:T(1,128)}, bf16[4096,16]{1,0:T(8,128)(2,1)}) custom-call(f32[4,6400,512]{2,1,0:T(8,128)} %train.1, bf16[4,6400,512]{2,1,0:T(8,128)(2,1)} %other.1, f32[4,512]{1,0:T(4,128)} %bitcast.2, f32[1,512]{1,0:T(1,128)} %bitcast.3), custom_call_target="tpu_custom_call" | custom-call | tf_op jit(solution)/shard_map/pallas_call | solution.py:221
  587.1 0.8 reduce
  587.8 0.7 reshape.9
  588.5 2.2 copy.7
  590.7 17.9 %copy.9 = bf16[4,800,4096]{2,1,0:T(8,128)(2,1)} copy(bf16[4,800,4096]{2,1,0:T(8,128)(2,1)} %get-tuple-element.15) | data formatting | bytes 52428800
where the time goes:
time: 609 us
  Pallas kernels  586 us (96%)
  local copies, waits for them, and re-layouts  20.8 us (3%)
    pallas_call x1, Pallas kernels, per_device(): pl.pallas_call(functools.partial(kernel, groups, shards, parts), out_shap...  586 us
    unnamed x2, local copies, waits for them, and re-layouts  20.1 us

commit v1 on v0

v1 whole, which is shorter than its diff:
```python
import functools

import jax
import jax.numpy as jnp
from jax import lax
from jax.experimental import pallas as pl
from jax.experimental.pallas import tpu as pltpu
from jax.sharding import PartitionSpec as P

MESH = pl.DeviceIdType.MESH
AHEAD = 3
DEPTH = 10
LANES = 128


def exchange(
    groups, shards, parts, direct,
    train, other, router, gain,
    ready, scale_out, serve,
    tbuf, obuf, stage, lmax, amax, rmax, hown, xmax, gown, gmax, rparts, rflip,
    tsem, osem, data_send, data_recv, a_send, a_recv,
    p1_send, p1_recv, p2_send, p2_recv, p3_send, p3_recv,
    r1_send, r1_recv, r2_send, r2_recv, r3_send, r3_recv,
):
    me = lax.axis_index("shard")
    group = lax.axis_index("expert")
    experts = train.shape[0]
    slots, _, rows, cols = tbuf.shape
    depth = stage.shape[0]
    chunks = experts * parts
    block = rows * parts
    half = shards // 2
    side, seat = me // half, lax.rem(me, half)

    def shard_id(k):
        return lax.rem(me + k, shards)

    def group_id(k):
        return lax.rem(group + k, groups)

    def seat_id(k):
        return lax.rem(seat + k, half)

    across = lax.rem(me + half, shards)

    barrier = pltpu.get_barrier_semaphore()
    for k in range(1, shards):
        pl.semaphore_signal(barrier, inc=1, device_id=(group, shard_id(k)), device_id_type=MESH)
    for k in range(1, groups):
        pl.semaphore_signal(barrier, inc=1, device_id=(group_id(k), me), device_id_type=MESH)

    def place(c, d):
        return c // parts, pl.ds(pl.multiple_of(d * block + lax.rem(c, parts) * rows, 8), rows)

    def load(c, d):
        e, span = place(c, d)
        slot = lax.rem(c, slots)
        return (
            pltpu.make_async_copy(train.at[e, span], tbuf.at[slot, d], tsem.at[slot, d]),
            pltpu.make_async_copy(other.at[e, span], obuf.at[slot, d], osem.at[slot, d]),
        )

    def start_load(c):
        def one(d, _):
            for copy in load(c, d):
                copy.start()
            return 0
        lax.fori_loop(0, shards, one, 0)

    def columns_of(d):
        return pl.ds(pl.multiple_of(d * cols, LANES), cols)

    def send(src, dst, send_sem, recv_sem, peer):
        return pltpu.make_async_remote_copy(
            src_ref=src, dst_ref=dst, send_sem=send_sem, recv_sem=recv_sem,
            device_id=(group, peer), device_id_type=MESH,
        )

    def wait_for(some, sem):
        pltpu.make_async_copy(some, some, sem).wait()

    def find_max(c):
        slot = lax.rem(c, slots)

        def one(d, _):
            for copy in load(c, d):
                copy.wait()
            best = None
            for j in range(0, cols, LANES):
                at = pl.ds(j, LANES)
                now = jnp.abs(tbuf[slot, d, :, at] + obuf[slot, d, :, at].astype(jnp.float32))
                best = now if best is None else jnp.maximum(best, now)
            lmax[c, d // half, lax.rem(d, half)] = jnp.max(best.T, axis=0, keepdims=True)
            return 0
        lax.fori_loop(0, shards, one, 0)

    def tell_all(c):
        def tell(k, _):
            send(lmax.at[c], amax.at[c, me], a_send.at[c], a_recv.at[c], shard_id(k)).start()
            return 0
        lax.fori_loop(1, shards, tell, 0)
        amax[c, me] = lmax[c]

    def hear_all(c):
        wait_for(amax.at[c, pl.ds(0, shards - 1)], a_recv.at[c])
        best = amax[c, 0]
        for d in range(1, shards):
            best = jnp.maximum(best, amax[c, d])
        for j in range(half):
            gmax[c, j] = best[:, j]

    def tell_leaders(c):
        def tell(k, _):
            j = seat_id(k)
            send(lmax.at[c, :, j], rmax.at[c, seat], p1_send.at[c], p1_recv.at[c], side * half + j).start()
            return 0
        lax.fori_loop(1, half, tell, 0)
        rmax[c, seat] = lmax[c, :, seat]

    def tell_across(c):
        wait_for(rmax.at[c, pl.ds(0, half - 1)], p1_recv.at[c])
        best = rmax[c, 0]
        for j in range(1, half):
            best = jnp.maximum(best, rmax[c, j])
        hown[c] = best
        send(hown.at[c], xmax.at[c], p2_send.at[c], p2_recv.at[c], across).start()

    def tell_half(c):
        wait_for(xmax.at[c], p2_recv.at[c])
        best = jnp.maximum(hown[c], xmax[c])
        gown[c] = best

        def tell(k, _):
            send(gown.at[c], gmax.at[c, seat], p3_send.at[c], p3_recv.at[c], side * half + seat_id(k)).start()
            return 0
        lax.fori_loop(1, half, tell, 0)
        gmax[c, seat] = best

    def narrow(c):
        slot = lax.rem(c, slots)
        berth = lax.rem(c, depth)
        e = c // parts
        span = pl.ds(pl.multiple_of(lax.rem(c, parts) * rows, 8), rows)

        @pl.when(c < direct)
        def _():
            hear_all(c)

        @pl.when(c >= direct)
        def _():
            wait_for(gmax.at[c, pl.ds(0, half - 1)], p3_recv.at[c])

        @pl.when(c >= depth)
        def _():
            wait_for(stage.at[berth, pl.ds(0, shards - 1)], data_send.at[berth])
        scale_out[c] = gmax[c, seat, side]

        def one(k, _):
            d = lax.rem(me + half + k, shards)
            tall = jnp.broadcast_to(gmax[c, lax.rem(d, half), d // half], (LANES, rows)).T
            for j in range(0, cols, LANES):
                at = pl.ds(j, LANES)
                now = tbuf[slot, d, :, at] + obuf[slot, d, :, at].astype(jnp.float32)
                stage[berth, d, :, at] = (now / tall).astype(jnp.bfloat16)

            @pl.when(d != me)
            def _():
                send(
                    stage.at[berth, d], ready.at[e, span, columns_of(me)],
                    data_send.at[berth], data_recv.at[me], d,
                ).start()

            @pl.when(d == me)
            def _():
                ready[e, span, columns_of(me)] = stage[berth, me]
            return 0
        lax.fori_loop(0, shards, one, 0)

    for c in range(direct):
        start_load(c)
    for c in range(direct):
        find_max(c)
    for c in range(direct, min(AHEAD + 2, chunks)):
        start_load(c)
    rparts[group, side, seat] = router[...] * gain[...]
    pl.semaphore_wait(barrier, shards - 1 + groups - 1)
    for c in range(direct):
        tell_all(c)
    mine = rparts.at[group, side, seat]
    send(mine, mine, r1_send, r1_recv, across).start()

    def step(c, _):
        @pl.when(c < chunks)
        def _():
            find_max(c)
            tell_leaders(c)

        @pl.when((c >= direct + 1) & (c <= chunks))
        def _():
            tell_across(c - 1)

        @pl.when((c >= direct + 2) & (c <= chunks + 1))
        def _():
            tell_half(c - 2)

        @pl.when(c == AHEAD)
        def _():
            wait_for(mine, r1_recv)
            for k in range(1, half):
                both = rparts.at[group, :, seat]
                send(both, both, r2_send, r2_recv, side * half + seat_id(k)).start()

        @pl.when(c == min(AHEAD + 1, chunks + AHEAD - 1))
        def _():
            wait_for(rparts.at[group, :, pl.ds(0, half - 1)], r2_recv)
            for k in range(1, groups):
                pltpu.make_async_remote_copy(
                    src_ref=rparts.at[group], dst_ref=rparts.at[group], send_sem=r3_send, recv_sem=r3_recv,
                    device_id=(group_id(k), me), device_id_type=MESH,
                ).start()

        narrow(c - AHEAD)

        @pl.when(c + 2 < chunks)
        def _():
            start_load(c + 2)
        return 0

    lax.fori_loop(AHEAD, chunks + AHEAD, step, 0)

    wait_for(rparts.at[pl.ds(0, groups - 1)], r3_recv)
    wide = router.shape[1]
    for d in range(shards):
        for g in range(groups):
            rflip[g * experts:(g + 1) * experts, :] = rparts[g, d // half, d % half]
        serve[:, d * wide:(d + 1) * wide] = rflip[...].astype(jnp.bfloat16)

    wait_for(mine, r1_send)
    wait_for(rparts.at[group, :, pl.ds(0, half - 1)], r2_send)
    wait_for(rparts.at[pl.ds(0, groups - 1)], r3_send)
    for c in range(direct):
        wait_for(amax.at[c, pl.ds(0, shards - 1)], a_send.at[c])

    def drain(c, _):
        wait_for(rmax.at[c, pl.ds(0, half - 1)], p1_send.at[c])
        wait_for(xmax.at[c], p2_send.at[c])
        wait_for(gmax.at[c, pl.ds(0, half - 1)], p3_send.at[c])
        return 0
    lax.fori_loop(direct, chunks, drain, 0)

    def unload(berth, _):
        wait_for(stage.at[berth, pl.ds(0, shards - 1)], data_send.at[berth])
        return 0
    lax.fori_loop(0, min(depth, chunks), unload, 0)

    def finish(k, _):
        d = shard_id(k)
        wait_for(ready.at[:, :, columns_of(d)], data_recv.at[d])
        return 0
    lax.fori_loop(1, shards, finish, 0)


def write_out(parts, landed, scale_in, serve_in, ready, scale, serve, sem):
    experts, block, _ = landed.shape
    rows = block // parts
    for e in range(experts):
        for p in range(parts):
            span = pl.ds(p * rows, rows)
            pltpu.make_async_copy(landed.at[e, span], ready.at[e, span], sem).start()
    serve[...] = serve_in[...]
    for e in range(experts):
        scale[e:e + 1, :] = jnp.concatenate([scale_in[e * parts + p] for p in range(parts)], axis=1)
    pltpu.make_async_copy(landed, ready, sem).wait()


def pieces(block):
    for count in (5, 4, 3, 2):
        if block % (16 * count) == 0:
            return count
    return 1


def per_device(groups, shards, train_down, other_down, router_weight, router_gain):
    experts, height, cols = train_down.shape
    block = height // shards
    parts = pieces(block)
    rows = block // parts
    chunks = experts * parts
    direct = min(AHEAD, chunks)
    slots = AHEAD + 2
    depth = min(DEPTH, chunks)
    half = shards // 2
    wide = router_weight.shape[0]
    f32, bf16 = jnp.float32, jnp.bfloat16
    dma = pltpu.SemaphoreType.DMA
    hbm = pl.BlockSpec(memory_space=pl.ANY)
    vmem = pl.BlockSpec(memory_space=pltpu.VMEM)
    landed, scale, serve = pl.pallas_call(
        functools.partial(exchange, groups, shards, parts, direct),
        out_shape=(
            pltpu.VMEM((experts, block, cols * shards), bf16),
            pltpu.VMEM((chunks, 1, rows), f32),
            pltpu.VMEM((experts * groups, wide * shards), bf16),
        ),
        in_specs=[hbm, hbm, vmem, vmem],
        out_specs=(vmem, vmem, vmem),
        scratch_shapes=[
            pltpu.VMEM((slots, shards, rows, cols), f32),
            pltpu.VMEM((slots, shards, rows, cols), bf16),
            pltpu.VMEM((depth, shards, rows, cols), bf16),
            pltpu.VMEM((chunks, 2, half, 1, rows), f32),
            pltpu.VMEM((direct, shards, 2, half, 1, rows), f32),
            pltpu.VMEM((chunks, half, 2, 1, rows), f32),
            pltpu.VMEM((chunks, 2, 1, rows), f32),
            pltpu.VMEM((chunks, 2, 1, rows), f32),
            pltpu.VMEM((chunks, 2, 1, rows), f32),
            pltpu.VMEM((chunks, half, 2, 1, rows), f32),
            pltpu.VMEM((groups, 2, half, experts, wide), f32),
            pltpu.VMEM((groups * experts, wide), f32),
            dma((slots, shards)), dma((slots, shards)),
            dma((depth,)), dma((shards,)),
            dma((direct,)), dma((direct,)),
            dma((chunks,)), dma((chunks,)), dma((chunks,)), dma((chunks,)), dma((chunks,)), dma((chunks,)),
            dma(()), dma(()), dma(()), dma(()), dma(()), dma(()),
        ],
        compiler_params=pltpu.CompilerParams(
            collective_id=0, has_side_effects=True, vmem_limit_bytes=36 * 2**20
        ),
    )(train_down, other_down, router_weight.T, router_gain[None, :])
    ready, scale, serve = pl.pallas_call(
        functools.partial(write_out, parts),
        out_shape=(
            jax.ShapeDtypeStruct((experts, block, cols * shards), bf16),
            jax.ShapeDtypeStruct((experts, block), f32),
            jax.ShapeDtypeStruct((experts * groups, wide * shards), bf16),
        ),
        in_specs=[vmem, vmem, vmem],
        out_specs=(hbm, vmem, vmem),
        scratch_shapes=[dma(())],
        compiler_params=pltpu.CompilerParams(vmem_limit_bytes=8 * 2**20),
    )(landed, scale, serve)
    return ready, scale, serve.T


def solution(mesh):
    in_specs = (
        P("expert", None, "shard"),
        P("expert", None, "shard"),
        P("shard", "expert"),
        P("shard"),
    )
    out_specs = (P("expert", "shard", None), P("expert", "shard"), P())
    body = functools.partial(per_device, mesh.shape["expert"], mesh.shape["shard"])
    return jax.shard_map(
        body, mesh=mesh, in_specs=in_specs, out_specs=out_specs, check_vma=False
    )
```

time: 609 us -> 592 us (0.972)
  local copies, waits for them, and re-layouts: 20.8 us -> 0 us
    unnamed x2 -> x0, local copies, waits for them, and re-layouts: 20.1 us -> none
    pallas_call x1 -> x2, Pallas kernels: 586 us -> 591 us  [the longest x1 582 us: per_device(): pl.pallas_call(functools.partial(exchange, groups, shards, parts, direct)...]
where the time goes in v1:
time: 592 us
  Pallas kernels  591 us (100%)
    pallas_call x1, Pallas kernels, per_device(): pl.pallas_call(functools.partial(exchange, groups, shards, parts, direct)...  582 us

profile of v1, /device:TPU:0, one launch (start us, length us, event | category | flops | bytes accessed | tf_op | source)
XLA Modules:
  0.0 591.9 jit_solution(15914971634985916125)
XLA Ops:
  0.6 581.9 %shard_map.67 = (bf16[4,800,4096]{2,1,0:T(8,128)(2,1)S(1)}, f32[20,1,160]{2,1,0:T(1,128)S(1)}, bf16[16,4096]{1,0:T(8,128)(2,1)S(1)}) custom-call(f32[4,6400,512]{2,1,0:T(8,128)} %train.1, bf16[4,6400,512]{2,1,0:T(8,128)(2,1)} %other.1, f32[4,512]{1,0:T(4,128)} %bitcast.3, f32[1,512]{1,0:T(1,128)} %bitcast.4), custom_call_target="tpu_custom_call" | custom-call | tf_op jit(solution)/shard_map/pallas_call | solution.py:298
  582.5 9.4 %shard_map.68 = (bf16[4,800,4096]{2,1,0:T(8,128)(2,1)}, f32[4,800]{1,0:T(4,128)}, bf16[16,4096]{1,0:T(8,128)(2,1)}) custom-call(bf16[4,800,4096]{2,1,0:T(8,128)(2,1)S(1)} %get-tuple-element.9.landed, f32[20,1,160]{2,1,0:T(1,128)S(1)} %get-tuple-element.10.scale_in, bf16[16,4096]{1,0:T(8,128)(2,1)S(1)} %get-tuple-element.11.serve_in), custom_call_target="tpu_custom_call" | custom-call | tf_op jit(solution)/shard_map/pallas_call | solution.py:330

commit v2 on v1

--- a/solution.py
+++ b/solution.py
@@ -10,13 +10,14 @@
 MESH = pl.DeviceIdType.MESH
 AHEAD = 3
 DEPTH = 10
+LATE = 192
 LANES = 128
 
 
 def exchange(
-    groups, shards, parts, direct,
+    groups, shards, parts, direct, late,
     train, other, router, gain,
-    ready, scale_out, serve,
+    ready, scale_out, serve, last,
     tbuf, obuf, stage, lmax, amax, rmax, hown, xmax, gown, gmax, rparts, rflip,
     tsem, osem, data_send, data_recv, a_send, a_recv,
     p1_send, p1_recv, p2_send, p2_recv, p3_send, p3_recv,
@@ -27,6 +28,7 @@
     experts = train.shape[0]
     slots, _, rows, cols = tbuf.shape
     depth = stage.shape[0]
+    total = experts * parts * rows
     chunks = experts * parts
     block = rows * parts
     half = shards // 2
@@ -42,6 +44,16 @@
         return lax.rem(seat + k, half)
 
     across = lax.rem(me + half, shards)
+    kept = {}
+    for c in range(chunks - 1, -1, -1):
+        left = max(0, min(rows, total - late - c * rows))
+        if left < rows:
+            kept[c] = left
+
+    def held(c, b):
+        if c in kept:
+            return stage.at[b, pl.ds(0, (shards - 2) * rows + kept[c])]
+        return stage.at[b, pl.ds(0, (shards - 1) * rows)]
 
     barrier = pltpu.get_barrier_semaphore()
     for k in range(1, shards):
@@ -139,8 +151,7 @@
     def narrow(c):
         slot = lax.rem(c, slots)
         berth = lax.rem(c, depth)
-        e = c // parts
-        span = pl.ds(pl.multiple_of(lax.rem(c, parts) * rows, 8), rows)
+        first = pl.multiple_of(c * rows, 8)
 
         @pl.when(c < direct)
         def _():
@@ -152,7 +163,7 @@
 
         @pl.when(c >= depth)
         def _():
-            wait_for(stage.at[berth, pl.ds(0, shards - 1)], data_send.at[berth])
+            wait_for(held(None, berth), data_send.at[berth])
         scale_out[c] = gmax[c, seat, side]
 
         def one(k, _):
@@ -161,18 +172,34 @@
             for j in range(0, cols, LANES):
                 at = pl.ds(j, LANES)
                 now = tbuf[slot, d, :, at] + obuf[slot, d, :, at].astype(jnp.float32)
-                stage[berth, d, :, at] = (now / tall).astype(jnp.bfloat16)
-
-            @pl.when(d != me)
-            def _():
+                stage[berth, pl.ds(pl.multiple_of(d * rows, 8), rows), at] = (now / tall).astype(jnp.bfloat16)
+
+            def part(count):
                 send(
-                    stage.at[berth, d], ready.at[e, span, columns_of(me)],
+                    stage.at[berth, pl.ds(pl.multiple_of(d * rows, 8), count)],
+                    ready.at[pl.ds(first, count), columns_of(me)],
                     data_send.at[berth], data_recv.at[me], d,
                 ).start()
 
+            whole = d != me
+            for special in kept:
+                whole = whole & ((k > 0) | (c != special))
+
+            @pl.when(whole)
+            def _():
+                part(rows)
+
+            for special, left in kept.items():
+                @pl.when((k == 0) & (c == special))
+                def _():
+                    if left:
+                        part(left)
+                    at = special * rows + left - (total - late)
+                    last[at:at + rows - left, :] = stage[berth, pl.ds(pl.multiple_of(d * rows + left, 8), rows - left), :]
+
             @pl.when(d == me)
             def _():
-                ready[e, span, columns_of(me)] = stage[berth, me]
+                ready[pl.ds(first, rows), columns_of(me)] = stage[berth, pl.ds(pl.multiple_of(d * rows, 8), rows), :]
             return 0
         lax.fori_loop(0, shards, one, 0)
 
@@ -248,29 +275,45 @@
         return 0
     lax.fori_loop(direct, chunks, drain, 0)
 
-    def unload(berth, _):
-        wait_for(stage.at[berth, pl.ds(0, shards - 1)], data_send.at[berth])
-        return 0
-    lax.fori_loop(0, min(depth, chunks), unload, 0)
+    for c in range(chunks - depth, chunks):
+        wait_for(held(c, c % depth), data_send.at[c % depth])
+
+    wait_for(ready.at[pl.ds(0, total - late), columns_of(across)], data_recv.at[across])
 
     def finish(k, _):
-        d = shard_id(k)
-        wait_for(ready.at[:, :, columns_of(d)], data_recv.at[d])
+        d = lax.rem(across + k, shards)
+
+        @pl.when(d != me)
+        def _():
+            wait_for(ready.at[:, columns_of(d)], data_recv.at[d])
         return 0
     lax.fori_loop(1, shards, finish, 0)
 
 
-def write_out(parts, landed, scale_in, serve_in, ready, scale, serve, sem):
-    experts, block, _ = landed.shape
+def write_out(parts, landed, scale_in, serve_in, ready, scale, serve, rows_of, sem, scale_sem, serve_sem):
+    experts, block, _ = ready.shape
     rows = block // parts
     for e in range(experts):
-        for p in range(parts):
-            span = pl.ds(p * rows, rows)
-            pltpu.make_async_copy(landed.at[e, span], ready.at[e, span], sem).start()
-    serve[...] = serve_in[...]
+        pltpu.make_async_copy(landed.at[pl.ds(e * block, block)], ready.at[e], sem.at[e]).start()
+    pltpu.make_async_copy(serve_in, serve, serve_sem).start()
     for e in range(experts):
-        scale[e:e + 1, :] = jnp.concatenate([scale_in[e * parts + p] for p in range(parts)], axis=1)
-    pltpu.make_async_copy(landed, ready, sem).wait()
+        rows_of[e:e + 1, :] = jnp.concatenate([scale_in[e * parts + p] for p in range(parts)], axis=1)
+    pltpu.make_async_copy(rows_of, scale, scale_sem).start()
+    pltpu.make_async_copy(serve_in, serve, serve_sem).wait()
+    pltpu.make_async_copy(rows_of, scale, scale_sem).wait()
+    for e in range(experts):
+        pltpu.make_async_copy(landed.at[pl.ds(e * block, block)], ready.at[e], sem.at[e]).wait()
+
+
+def add_last(shards, ready_in, last, ready, sem):
+    late, cols = last.shape
+    experts, block, _ = ready.shape
+    across = lax.rem(lax.axis_index("shard") + shards // 2, shards)
+    copy = pltpu.make_async_copy(
+        last, ready.at[experts - 1, pl.ds(block - late, late), pl.ds(pl.multiple_of(across * cols, LANES), cols)], sem
+    )
+    copy.start()
+    copy.wait()
 
 
 def pieces(block):
@@ -291,23 +334,25 @@
     depth = min(DEPTH, chunks)
     half = shards // 2
     wide = router_weight.shape[0]
+    late = LATE if chunks > depth and LATE < block else 0
     f32, bf16 = jnp.float32, jnp.bfloat16
     dma = pltpu.SemaphoreType.DMA
     hbm = pl.BlockSpec(memory_space=pl.ANY)
     vmem = pl.BlockSpec(memory_space=pltpu.VMEM)
-    landed, scale, serve = pl.pallas_call(
-        functools.partial(exchange, groups, shards, parts, direct),
+    landed, scale, serve, last = pl.pallas_call(
+        functools.partial(exchange, groups, shards, parts, direct, late),
         out_shape=(
-            pltpu.VMEM((experts, block, cols * shards), bf16),
+            pltpu.VMEM((experts * block, cols * shards), bf16),
             pltpu.VMEM((chunks, 1, rows), f32),
             pltpu.VMEM((experts * groups, wide * shards), bf16),
+            pltpu.VMEM((max(late, 16), cols), bf16),
         ),
         in_specs=[hbm, hbm, vmem, vmem],
-        out_specs=(vmem, vmem, vmem),
+        out_specs=(vmem, vmem, vmem, vmem),
         scratch_shapes=[
             pltpu.VMEM((slots, shards, rows, cols), f32),
             pltpu.VMEM((slots, shards, rows, cols), bf16),
-            pltpu.VMEM((depth, shards, rows, cols), bf16),
+            pltpu.VMEM((depth, shards * rows, cols), bf16),
             pltpu.VMEM((chunks, 2, half, 1, rows), f32),
             pltpu.VMEM((direct, shards, 2, half, 1, rows), f32),
             pltpu.VMEM((chunks, half, 2, 1, rows), f32),
@@ -327,6 +372,9 @@
             collective_id=0, has_side_effects=True, vmem_limit_bytes=36 * 2**20
         ),
     )(train_down, other_down, router_weight.T, router_gain[None, :])
+    if late:
+        swap = [(d, (d + half) % shards) for d in range(shards)]
+        last = lax.ppermute(last, "shard", swap)
     ready, scale, serve = pl.pallas_call(
         functools.partial(write_out, parts),
         out_shape=(
@@ -335,10 +383,21 @@
             jax.ShapeDtypeStruct((experts * groups, wide * shards), bf16),
         ),
         in_specs=[vmem, vmem, vmem],
-        out_specs=(hbm, vmem, vmem),
-        scratch_shapes=[dma(())],
-        compiler_params=pltpu.CompilerParams(vmem_limit_bytes=8 * 2**20),
+        out_specs=(hbm, hbm, hbm),
+        scratch_shapes=[pltpu.VMEM((experts, block), f32), dma((experts,)), dma(()), dma(())],
+        cost_estimate=pl.CostEstimate(flops=0, bytes_accessed=4 * experts * block * cols * shards, transcendentals=0),
+        compiler_params=pltpu.CompilerParams(vmem_limit_bytes=4 * 2**20),
     )(landed, scale, serve)
+    if late:
+        ready = pl.pallas_call(
+            functools.partial(add_last, shards),
+            out_shape=jax.ShapeDtypeStruct(ready.shape, bf16),
+            in_specs=[hbm, vmem],
+            out_specs=hbm,
+            input_output_aliases={0: 0},
+            scratch_shapes=[dma(())],
+            compiler_params=pltpu.CompilerParams(vmem_limit_bytes=4 * 2**20),
+        )(ready, last)
     return ready, scale, serve.T
 
 

time: 592 us -> 586 us (0.990)
  Pallas kernels: 591 us -> 583 us
    pallas_call x1 -> x2, Pallas kernels: 582 us -> 574 us  [the longest x1 573 us: per_device(): pl.pallas_call(functools.partial(exchange, groups, shards, parts, direct,...]
  transfers between devices with their start and end apart: 0 -> 1, of which waited for: 0 -> 1; matrix products, arithmetic and copies ran while one was open for 0% -> 0% of each run, Pallas kernels for 0% -> 2%
where the time goes in v2:
time: 586 us
  Pallas kernels  583 us (99%)
    pallas_call x1, Pallas kernels, per_device(): pl.pallas_call(functools.partial(exchange, groups, shards, parts, direct,...  573 us
  transfers between devices with their start and end apart: 1, of which 1 were waited for; matrix products, arithmetic and copies ran while one was open for 0% of the time, Pallas kernels for 2%

profile of v2, /device:TPU:0, one launch (start us, length us, event | category | flops | bytes accessed | tf_op | source)
XLA Modules:
  0.0 586.1 jit_solution(9802616156747655310)
XLA Ops:
  0.6 573.5 %shard_map.67 = (bf16[3200,4096]{1,0:T(8,128)(2,1)S(1)}, f32[20,1,160]{2,1,0:T(1,128)S(1)}, bf16[16,4096]{1,0:T(8,128)(2,1)S(1)}, bf16[192,512]{1,0:T(8,128)(2,1)S(1)}) custom-call(f32[4,6400,512]{2,1,0:T(8,128)} %train.1, bf16[4,6400,512]{2,1,0:T(8,128)(2,1)} %other.1, f32[4,512]{1,0:T(4,128)} %bitcast.3, f32[1,512]{1,0:T(1,128)} %bitcast.4), custom_call_target="tpu_custom_call" | custom-call | tf_op jit(solution)/shard_map/pallas_call | solution.py:342
  574.1 0.1 collective-permute-start
  574.2 9.0 %shard_map.68 = (bf16[4,800,4096]{2,1,0:T(8,128)(2,1)}, f32[4,800]{1,0:T(4,128)}, bf16[16,4096]{1,0:T(8,128)(2,1)}) custom-call(bf16[3200,4096]{1,0:T(8,128)(2,1)S(1)} %get-tuple-element.10.landed, f32[20,1,160]{2,1,0:T(1,128)S(1)} %get-tuple-element.11.scale_in, bf16[16,4096]{1,0:T(8,128)(2,1)S(1)} %get-tuple-element.12.serve_in), custom_call_target="tpu_custom_call" | custom-call | bytes 52428800 | tf_op jit(solution)/shard_map/pallas_call | solution.py:378
  583.2 2.2 collective-permute-done.last
  585.4 0.7 shard_map.69
Async XLA Ops:
  574.1 11.3 %collective-permute-start = (bf16[192,512]{1,0:T(8,128)(2,1)S(1)}, bf16[192,512]{1,0:T(8,128)(2,1)S(1)}, u32[]{:S(2)}, u32[]{:S(2)}) collective-permute-start(bf16[192,512]{1,0:T(8,128)(2,1)S(1)} %get-tuple-element.14), channel_id=1, source_target_pairs={{0,4},{1,5},{2,6},{3,7},{4,0},{5,1},{6,2},{7,3},{8,12},{9,13},{10,... | collective-permute-start | bytes 589832 | tf_op jit(solution)/shard_map/ppermute | solution.py:377

commit v3 on v2

--- a/solution.py
+++ b/solution.py
@@ -10,6 +10,8 @@
 MESH = pl.DeviceIdType.MESH
 AHEAD = 3
 DEPTH = 10
+SOON = 2
+EARLY = 2
 LATE = 192
 LANES = 128
 
@@ -148,26 +150,29 @@
         lax.fori_loop(1, half, tell, 0)
         gmax[c, seat] = best
 
-    def narrow(c):
+    def open_chunk(c):
+        berth = lax.rem(c, depth)
+
+        @pl.when(c < direct)
+        def _():
+            hear_all(c)
+
+        @pl.when(c >= direct)
+        def _():
+            wait_for(gmax.at[c, pl.ds(0, half - 1)], p3_recv.at[c])
+
+        @pl.when(c >= depth)
+        def _():
+            wait_for(held(None, berth), data_send.at[berth])
+        scale_out[c] = gmax[c, seat, side]
+
+    def narrow(c, begin, end):
         slot = lax.rem(c, slots)
         berth = lax.rem(c, depth)
         first = pl.multiple_of(c * rows, 8)
 
-        @pl.when(c < direct)
-        def _():
-            hear_all(c)
-
-        @pl.when(c >= direct)
-        def _():
-            wait_for(gmax.at[c, pl.ds(0, half - 1)], p3_recv.at[c])
-
-        @pl.when(c >= depth)
-        def _():
-            wait_for(held(None, berth), data_send.at[berth])
-        scale_out[c] = gmax[c, seat, side]
-
         def one(k, _):
-            d = lax.rem(me + half + k, shards)
+            d = lax.rem(me + half + half * lax.rem(c, 2) + k, shards)
             tall = jnp.broadcast_to(gmax[c, lax.rem(d, half), d // half], (LANES, rows)).T
             for j in range(0, cols, LANES):
                 at = pl.ds(j, LANES)
@@ -183,14 +188,14 @@
 
             whole = d != me
             for special in kept:
-                whole = whole & ((k > 0) | (c != special))
+                whole = whole & ((d != across) | (c != special))
 
             @pl.when(whole)
             def _():
                 part(rows)
 
             for special, left in kept.items():
-                @pl.when((k == 0) & (c == special))
+                @pl.when((d == across) & (c == special))
                 def _():
                     if left:
                         part(left)
@@ -201,20 +206,24 @@
             def _():
                 ready[pl.ds(first, rows), columns_of(me)] = stage[berth, pl.ds(pl.multiple_of(d * rows, 8), rows), :]
             return 0
-        lax.fori_loop(0, shards, one, 0)
+        lax.fori_loop(begin, end, one, 0)
 
     for c in range(direct):
         start_load(c)
-    for c in range(direct):
+    for c in range(min(SOON, direct)):
         find_max(c)
     for c in range(direct, min(AHEAD + 2, chunks)):
         start_load(c)
     rparts[group, side, seat] = router[...] * gain[...]
     pl.semaphore_wait(barrier, shards - 1 + groups - 1)
     for c in range(direct):
+        if c >= SOON:
+            find_max(c)
         tell_all(c)
     mine = rparts.at[group, side, seat]
     send(mine, mine, r1_send, r1_recv, across).start()
+    open_chunk(0)
+    narrow(0, 0, EARLY)
 
     def step(c, _):
         @pl.when(c < chunks)
@@ -246,7 +255,10 @@
                     device_id=(group_id(k), me), device_id_type=MESH,
                 ).start()
 
-        narrow(c - AHEAD)
+        @pl.when(c > AHEAD)
+        def _():
+            open_chunk(c - AHEAD)
+        narrow(c - AHEAD, jnp.where(c == AHEAD, EARLY, 0), shards)
 
         @pl.when(c + 2 < chunks)
         def _():

time: 586 us -> 582 us (level)
  Pallas kernels: 583 us -> 575 us
    pallas_call x1, Pallas kernels: 573 us -> 566 us  [per_device(): pl.pallas_call(functools.partial(exchange, groups, shards, parts, direct,...]
  transfers between devices with their start and end apart: 1 -> 1, of which waited for: 1 -> 0; matrix products, arithmetic and copies ran while one was open for 0% -> 0% of each run, Pallas kernels for 2% -> 2%
where the time goes in v3:
time: 582 us; the launch traced here: 581 us
  Pallas kernels  575 us (99%)
    pallas_call x1, Pallas kernels, per_device(): pl.pallas_call(functools.partial(exchange, groups, shards, parts, direct,...  566 us
  transfers between devices with their start and end apart: 1, of which 0 were waited for; matrix products, arithmetic and copies ran while one was open for 0% of the time, Pallas kernels for 2%

profile of v3, /device:TPU:0, one launch (start us, length us, event | category | flops | bytes accessed | tf_op | source)
XLA Modules:
  0.0 581.4 jit_solution(16653357468298978910)
XLA Ops:
  0.6 565.6 %shard_map.67 = (bf16[3200,4096]{1,0:T(8,128)(2,1)S(1)}, f32[20,1,160]{2,1,0:T(1,128)S(1)}, bf16[16,4096]{1,0:T(8,128)(2,1)S(1)}, bf16[192,512]{1,0:T(8,128)(2,1)S(1)}) custom-call(f32[4,6400,512]{2,1,0:T(8,128)} %train.1, bf16[4,6400,512]{2,1,0:T(8,128)(2,1)} %other.1, f32[4,512]{1,0:T(4,128)} %bitcast.3, f32[1,512]{1,0:T(1,128)} %bitcast.4), custom_call_target="tpu_custom_call" | custom-call | tf_op jit(solution)/shard_map/pallas_call | solution.py:354
  566.2 5.5 collective-permute-start
  571.7 9.0 %shard_map.68 = (bf16[4,800,4096]{2,1,0:T(8,128)(2,1)}, f32[4,800]{1,0:T(4,128)}, bf16[16,4096]{1,0:T(8,128)(2,1)}) custom-call(bf16[3200,4096]{1,0:T(8,128)(2,1)S(1)} %get-tuple-element.10.landed, f32[20,1,160]{2,1,0:T(1,128)S(1)} %get-tuple-element.11.scale_in, bf16[16,4096]{1,0:T(8,128)(2,1)S(1)} %get-tuple-element.12.serve_in), custom_call_target="tpu_custom_call" | custom-call | bytes 52428800 | tf_op jit(solution)/shard_map/pallas_call | solution.py:390
  580.7 0.0 collective-permute-done.last
  580.7 0.7 shard_map.69
Async XLA Ops:
  566.2 14.5 %collective-permute-start = (bf16[192,512]{1,0:T(8,128)(2,1)S(1)}, bf16[192,512]{1,0:T(8,128)(2,1)S(1)}, u32[]{:S(2)}, u32[]{:S(2)}) collective-permute-start(bf16[192,512]{1,0:T(8,128)(2,1)S(1)} %get-tuple-element.14), channel_id=1, source_target_pairs={{0,4},{1,5},{2,6},{3,7},{4,0},{5,1},{6,2},{7,3},{8,12},{9,13},{10,... | collective-permute-start | bytes 589832 | tf_op jit(solution)/shard_map/ppermute | solution.py:389

commit v4 on v3

--- a/solution.py
+++ b/solution.py
@@ -10,7 +10,8 @@
 MESH = pl.DeviceIdType.MESH
 AHEAD = 3
 DEPTH = 10
-SOON = 2
+DIRECT = 1
+SOON = 1
 EARLY = 2
 LATE = 192
 LANES = 128
@@ -208,20 +209,25 @@
             return 0
         lax.fori_loop(begin, end, one, 0)
 
-    for c in range(direct):
+    for c in range(min(AHEAD, chunks)):
         start_load(c)
-    for c in range(min(SOON, direct)):
+    for c in range(min(SOON, chunks)):
         find_max(c)
-    for c in range(direct, min(AHEAD + 2, chunks)):
+    for c in range(AHEAD, min(AHEAD + 2, chunks)):
         start_load(c)
     rparts[group, side, seat] = router[...] * gain[...]
     pl.semaphore_wait(barrier, shards - 1 + groups - 1)
-    for c in range(direct):
+    for c in range(min(AHEAD, chunks)):
         if c >= SOON:
             find_max(c)
-        tell_all(c)
+        if c < direct:
+            tell_all(c)
+        else:
+            tell_leaders(c)
     mine = rparts.at[group, side, seat]
     send(mine, mine, r1_send, r1_recv, across).start()
+    for c in range(direct, min(AHEAD - 1, chunks)):
+        tell_across(c)
     open_chunk(0)
     narrow(0, 0, EARLY)
 
@@ -231,7 +237,7 @@
             find_max(c)
             tell_leaders(c)
 
-        @pl.when((c >= direct + 1) & (c <= chunks))
+        @pl.when((c >= max(direct + 1, AHEAD)) & (c <= chunks))
         def _():
             tell_across(c - 1)
 
@@ -306,7 +312,9 @@
     experts, block, _ = ready.shape
     rows = block // parts
     for e in range(experts):
-        pltpu.make_async_copy(landed.at[pl.ds(e * block, block)], ready.at[e], sem.at[e]).start()
+        for p in range(parts):
+            span = pl.ds(p * rows, rows)
+            pltpu.make_async_copy(landed.at[pl.ds(e * block + p * rows, rows)], ready.at[e, span], sem.at[e]).start()
     pltpu.make_async_copy(serve_in, serve, serve_sem).start()
     for e in range(experts):
         rows_of[e:e + 1, :] = jnp.concatenate([scale_in[e * parts + p] for p in range(parts)], axis=1)
@@ -341,7 +349,7 @@
     parts = pieces(block)
     rows = block // parts
     chunks = experts * parts
-    direct = min(AHEAD, chunks)
+    direct = min(DIRECT, chunks)
     slots = AHEAD + 2
     depth = min(DEPTH, chunks)
     half = shards // 2

time: 582 us -> 581 us (level)
  transfers between devices with their start and end apart: 1 -> 1, of which waited for: 0 -> 1; matrix products, arithmetic and copies ran while one was open for 0% -> 0% of each run, Pallas kernels for 2% -> 2%
where the time goes in v4:
time: 581 us; the launch traced here: 580 us
  Pallas kernels  573 us (99%)
  starting transfers between devices  5.97 us (1%)
    pallas_call x1, Pallas kernels, per_device(): pl.pallas_call(functools.partial(exchange, groups, shards, parts, direct,...  564 us
  transfers between devices with their start and end apart: 1, of which 1 were waited for; matrix products, arithmetic and copies ran while one was open for 0% of the time, Pallas kernels for 2%

profile of v4, /device:TPU:0, one launch (start us, length us, event | category | flops | bytes accessed | tf_op | source)
XLA Modules:
  0.0 580.5 jit_solution(4219058633131591748)
XLA Ops:
  0.6 564.0 %shard_map.67 = (bf16[3200,4096]{1,0:T(8,128)(2,1)S(1)}, f32[20,1,160]{2,1,0:T(1,128)S(1)}, bf16[16,4096]{1,0:T(8,128)(2,1)S(1)}, bf16[192,512]{1,0:T(8,128)(2,1)S(1)}) custom-call(f32[4,6400,512]{2,1,0:T(8,128)} %train.1, bf16[4,6400,512]{2,1,0:T(8,128)(2,1)} %other.1, f32[4,512]{1,0:T(4,128)} %bitcast.3, f32[1,512]{1,0:T(1,128)} %bitcast.4), custom_call_target="tpu_custom_call" | custom-call | tf_op jit(solution)/shard_map/pallas_call | solution.py:362
  564.6 6.0 %collective-permute-start = (bf16[192,512]{1,0:T(8,128)(2,1)S(1)}, bf16[192,512]{1,0:T(8,128)(2,1)S(1)}, u32[]{:S(2)}, u32[]{:S(2)}) collective-permute-start(bf16[192,512]{1,0:T(8,128)(2,1)S(1)} %get-tuple-element.14), channel_id=1, source_target_pairs={{0,4},{1,5},{2,6},{3,7},{4,0},{5,1},{6,2},{7,3},{8,12},{9,13},{10,... | collective-permute-start | bytes 589832 | tf_op jit(solution)/shard_map/ppermute | solution.py:397
  570.6 8.7 %shard_map.68 = (bf16[4,800,4096]{2,1,0:T(8,128)(2,1)}, f32[4,800]{1,0:T(4,128)}, bf16[16,4096]{1,0:T(8,128)(2,1)}) custom-call(bf16[3200,4096]{1,0:T(8,128)(2,1)S(1)} %get-tuple-element.10.landed, f32[20,1,160]{2,1,0:T(1,128)S(1)} %get-tuple-element.11.scale_in, bf16[16,4096]{1,0:T(8,128)(2,1)S(1)} %get-tuple-element.12.serve_in), custom_call_target="tpu_custom_call" | custom-call | bytes 52428800 | tf_op jit(solution)/shard_map/pallas_call | solution.py:398
  579.4 0.4 collective-permute-done.last
  579.8 0.7 shard_map.69
Async XLA Ops:
  564.6 15.2 %collective-permute-start = (bf16[192,512]{1,0:T(8,128)(2,1)S(1)}, bf16[192,512]{1,0:T(8,128)(2,1)S(1)}, u32[]{:S(2)}, u32[]{:S(2)}) collective-permute-start(bf16[192,512]{1,0:T(8,128)(2,1)S(1)} %get-tuple-element.14), channel_id=1, source_target_pairs={{0,4},{1,5},{2,6},{3,7},{4,0},{5,1},{6,2},{7,3},{8,12},{9,13},{10,... | collective-permute-start | bytes 589832 | tf_op jit(solution)/shard_map/ppermute | solution.py:397

commit v5 on v4

--- a/solution.py
+++ b/solution.py
@@ -12,7 +12,7 @@
 DEPTH = 10
 DIRECT = 1
 SOON = 1
-EARLY = 2
+EARLY = 1
 LATE = 192
 LANES = 128
 

time: 581 us -> 581 us (level)
  no operation moved by 1% of the time
where the time goes in v5:
time: 581 us; the launch traced here: 580 us
  Pallas kernels  573 us (99%)
  starting transfers between devices  5.97 us (1%)
    pallas_call x1, Pallas kernels, per_device(): pl.pallas_call(functools.partial(exchange, groups, shards, parts, direct,...  564 us
  transfers between devices with their start and end apart: 1, of which 1 were waited for; matrix products, arithmetic and copies ran while one was open for 0% of the time, Pallas kernels for 2%

profile of v5, /device:TPU:0, one launch (start us, length us, event | category | flops | bytes accessed | tf_op | source)
XLA Modules:
  0.0 580.5 jit_solution(6939074523341715233)
XLA Ops:
  0.6 564.0 %shard_map.67 = (bf16[3200,4096]{1,0:T(8,128)(2,1)S(1)}, f32[20,1,160]{2,1,0:T(1,128)S(1)}, bf16[16,4096]{1,0:T(8,128)(2,1)S(1)}, bf16[192,512]{1,0:T(8,128)(2,1)S(1)}) custom-call(f32[4,6400,512]{2,1,0:T(8,128)} %train.1, bf16[4,6400,512]{2,1,0:T(8,128)(2,1)} %other.1, f32[4,512]{1,0:T(4,128)} %bitcast.3, f32[1,512]{1,0:T(1,128)} %bitcast.4), custom_call_target="tpu_custom_call" | custom-call | tf_op jit(solution)/shard_map/pallas_call | solution.py:362
  564.6 6.0 %collective-permute-start = (bf16[192,512]{1,0:T(8,128)(2,1)S(1)}, bf16[192,512]{1,0:T(8,128)(2,1)S(1)}, u32[]{:S(2)}, u32[]{:S(2)}) collective-permute-start(bf16[192,512]{1,0:T(8,128)(2,1)S(1)} %get-tuple-element.14), channel_id=1, source_target_pairs={{0,4},{1,5},{2,6},{3,7},{4,0},{5,1},{6,2},{7,3},{8,12},{9,13},{10,... | collective-permute-start | bytes 589832 | tf_op jit(solution)/shard_map/ppermute | solution.py:397
  570.6 8.7 %shard_map.68 = (bf16[4,800,4096]{2,1,0:T(8,128)(2,1)}, f32[4,800]{1,0:T(4,128)}, bf16[16,4096]{1,0:T(8,128)(2,1)}) custom-call(bf16[3200,4096]{1,0:T(8,128)(2,1)S(1)} %get-tuple-element.10.landed, f32[20,1,160]{2,1,0:T(1,128)S(1)} %get-tuple-element.11.scale_in, bf16[16,4096]{1,0:T(8,128)(2,1)S(1)} %get-tuple-element.12.serve_in), custom_call_target="tpu_custom_call" | custom-call | bytes 52428800 | tf_op jit(solution)/shard_map/pallas_call | solution.py:398
  579.3 0.4 collective-permute-done.last
  579.8 0.7 shard_map.69
Async XLA Ops:
  564.6 15.2 %collective-permute-start = (bf16[192,512]{1,0:T(8,128)(2,1)S(1)}, bf16[192,512]{1,0:T(8,128)(2,1)S(1)}, u32[]{:S(2)}, u32[]{:S(2)}) collective-permute-start(bf16[192,512]{1,0:T(8,128)(2,1)S(1)} %get-tuple-element.14), channel_id=1, source_target_pairs={{0,4},{1,5},{2,6},{3,7},{4,0},{5,1},{6,2},{7,3},{8,12},{9,13},{10,... | collective-permute-start | bytes 589832 | tf_op jit(solution)/shard_map/ppermute | solution.py:397
